TPU v7x, 256 devices: a whole 4x4x8 slice. The times are simulated.
256 devices in a mesh: row: 8 (over y, core), col: 32 (over z, x).
Axes of the slice: x: 4, y: 4, z: 8, core: 2. Of those that a mesh axis runs over, the one named last changes fastest.
Arguments:
- rhs: bfloat16 [6144, 6144], P('row', 'col'), may hold values from -6 to 6
- basis_left: bfloat16 [6144, 6144], P('col', 'row'), may hold values from -1 to 1, as said below
- basis_right: bfloat16 [6144, 6144], P('row', 'col'), may hold values from -1 to 1, as said below
- eig_left: float32 [6144], P('row'), may hold values from 0.1 to 4
- eig_right: float32 [6144], P('col'), may hold values from 0.1 to 4
Outputs:
- solution: bfloat16 [6144, 6144], P('col', 'row')
Inputs may be any that keep to these rules, and one draw needn't show every extreme that they name: `basis_left`: an orthogonal matrix drawn uniformly, rounded to bfloat16. `basis_right`: an orthogonal matrix drawn uniformly, rounded to bfloat16.
All inputs are finite; a program needn't handle non-finite values.
Results may differ from a plain program's by a relative error of at most 0.0085.
Values may be sent and summed in bfloat16 or wider, within the bound.
A program may use at most 64 MiB of HBM per device.

v0:
```python
import jax
import jax.numpy as jnp
from jax import lax
from jax.sharding import PartitionSpec as P


def laid_out(parts, dim):
    parts = jnp.moveaxis(parts, 0, dim)
    lengths = parts.shape
    return parts.reshape(*lengths[:dim], lengths[dim] * lengths[dim + 1], *lengths[dim + 2 :])


def sent_to_all(shard, axis):
    copies = jnp.broadcast_to(shard, (lax.axis_size(axis), *shard.shape))
    return lax.all_to_all(copies, axis, split_axis=0, concat_axis=0, tiled=True)


def gathered_copies(shard, axis, dim):
    return laid_out(sent_to_all(shard, axis), dim)


def in_blocks(shard, dim, peers):
    lengths = shard.shape
    parts = shard.reshape(*lengths[:dim], peers, lengths[dim] // peers, *lengths[dim + 1 :])
    return jnp.moveaxis(parts, dim, 0)


def sent_and_summed(shard, axis, dim):
    peers = lax.axis_size(axis)
    parts = lax.all_to_all(in_blocks(shard, dim, peers), axis, 0, 0, tiled=True)
    return jnp.sum(parts.astype(jnp.float32), axis=0)


def body(rhs, basis_left, basis_right, eig_left, eig_right):
    c_strip = gathered_copies(rhs, "row", 0)
    chosen = c_strip
    first = lax.dot_general(
        lax.all_gather(basis_left, "col", axis=0, tiled=True),
        chosen,
        (((0,), (0,)), ((), ())),
        preferred_element_type=jnp.float32,
    )
    projected = first.astype(jnp.bfloat16)
    right_strip = lax.all_gather(basis_right, "row", axis=0, tiled=True)
    chosen = right_strip
    second = jnp.dot(
        lax.all_gather(projected, "col", axis=1, tiled=True),
        chosen,
        preferred_element_type=jnp.float32,
    )
    scaled = (second / (eig_left[:, None] + eig_right[None, :])).astype(jnp.bfloat16)
    scaled_strip = lax.all_gather(scaled, "col", axis=1, tiled=True)
    chosen = scaled_strip
    half_turned = sent_and_summed(
        lax.dot_general(
            chosen, basis_left, (((0,), (1,)), ((), ())), preferred_element_type=jnp.float32
        ).astype(jnp.bfloat16),
        "row",
        0,
    ).astype(jnp.bfloat16)
    half_strip = gathered_copies(half_turned, "row", 0)
    chosen = half_strip
    turned = jnp.dot(
        lax.all_gather(basis_right, "col", axis=1, tiled=True),
        chosen,
        preferred_element_type=jnp.float32,
    )
    return turned.T.astype(jnp.bfloat16)


def solution(mesh):
    in_specs = (P("row", "col"), P("col", "row"), P("row", "col"), P("row"), P("col"))
    out_specs = P("col", "row")
    return jax.shard_map(body, mesh=mesh, in_specs=in_specs, out_specs=out_specs, check_vma=False)
```

profile of v0, /device:TPU:1, one launch (start us, length us, event | category | flops | bytes accessed | tf_op | source)
XLA Modules:
  0.0 472.5 jit_solution(11340699577800707060)
XLA Ops:
  6.5 0.7 all-gather.6.cloned.1.call-update
  7.3 0.7 all-gather.10.cloned.1.call-update
  8.0 0.0 all-gather.8.cloned.1.call-start
  8.1 1.1 broadcast_in_dim.8
  9.2 34.7 %all_to_all.15 = bf16[8,768,192]{1,2,0:T(8,128)(2,1)S(1)} all-to-all(bf16[8,768,192]{1,2,0:T(8,128)(2,1)S(1)} %broadcast_in_dim.8), channel_id=1, replica_groups=mesh['row'=8,'col'=32] {'row'}, dimensions={0} | all-to-all | bytes 4718592 | tf_op jit(solution)/shard_map/all_to_all | solution.py:15
  43.9 0.3 copy.15
  44.2 71.9 %all-gather.6.cloned.1.call-done = bf16[6144,768]{1,0:T(8,128)(2,1)} async-done(((bf16[192,768]{1,0:T(8,128)(2,1)}), bf16[6144,768]{1,0:T(8,128)(2,1)}) %all-gather.6.cloned.1.call-update) | async-done | bytes 9437200 | tf_op jit(solution)/shard_map/all_gather | solution.py:38
  116.1 6.4 %convolution_convert_fusion.1 = bf16[768,192]{0,1:T(8,128)(2,1)} fusion(bf16[6144,192]{0,1:T(8,128)(2,1)S(1)} %bitcast.19, bf16[6144,768]{1,0:T(8,128)(2,1)} %all-gather.6.cloned.1.call-done), kind=kOutput, calls=%fused_computation.2 | convolution fusion | flops 1812086784 | bytes 12091392 | tf_op jit(solution)/shard_map/dot_general | solution.py:37
  122.5 0.0 all-gather.12.cloned.1.call-start
  122.6 21.8 %all-gather.10.cloned.1.call-done = bf16[6144,192]{0,1:T(8,128)(2,1)} async-done(((bf16[768,192]{0,1:T(8,128)(2,1)}), bf16[6144,192]{0,1:T(8,128)(2,1)}) %all-gather.10.cloned.1.call-update) | async-done | bytes 2359312 | tf_op jit(solution)/shard_map/all_gather | solution.py:44
  144.3 105.2 %all-gather.8.cloned.1.call-done = bf16[768,6144]{0,1:T(8,128)(2,1)} async-done(((bf16[768,192]{0,1:T(8,128)(2,1)}), bf16[768,6144]{0,1:T(8,128)(2,1)}) %all-gather.8.cloned.1.call-update) | async-done | bytes 9437200 | tf_op jit(solution)/shard_map/all_gather | solution.py:47
  249.5 7.1 %fusion = bf16[768,192]{0,1:T(8,128)(2,1)} fusion(bf16[6144,192]{0,1:T(8,128)(2,1)} %all-gather.10.cloned.1.call-done, bf16[768,6144]{0,1:T(8,128)(2,1)} %all-gather.8.cloned.1.call-done, f32[192]{0:T(256)S(1)} %copy-done.2, f32[768]{0:T(1024)S(1)} %copy-done.1), kind=kOutput, calls=%fused_computation.5 | convolution fusion | flops 1812381696 | bytes 12095232 | tf_op jit(solution)/shard_map/dot_general | solution.py:46
  256.6 0.0 all-gather.14.cloned.1.call-start
  256.7 0.5 all-gather.14.cloned.1.call-update
  257.2 99.8 %all-gather.12.cloned.1.call-done = bf16[768,6144]{0,1:T(8,128)(2,1)} async-done(((bf16[768,192]{0,1:T(8,128)(2,1)}), bf16[768,6144]{0,1:T(8,128)(2,1)}) %all-gather.12.cloned.1.call-update) | async-done | bytes 9437200 | tf_op jit(solution)/shard_map/all_gather | solution.py:52
  357.0 6.9 %convolution_convert_fusion = bf16[6144,192]{0,1:T(8,128)(2,1)S(1)} fusion(bf16[768,6144]{0,1:T(8,128)(2,1)} %all-gather.12.cloned.1.call-done, bf16[192,768]{1,0:T(8,128)(2,1)S(1)} %copy-done), kind=kOutput, calls=%fused_computation | convolution fusion | flops 1813118976 | bytes 12091392 | tf_op jit(solution)/shard_map/dot_general | solution.py:55
  363.9 0.2 copy.18
  364.0 34.5 %all_to_all.16 = bf16[8,768,192]{1,2,0:T(8,128)(2,1)S(1)} all-to-all(bf16[8,768,192]{1,2,0:T(8,128)(2,1)S(1)} %bitcast.17), channel_id=1, replica_groups=mesh['row'=8,'col'=32] {'row'}, dimensions={0} | all-to-all | bytes 4718592 | tf_op jit(solution)/shard_map/all_to_all | solution.py:30
  398.5 0.4 reduce_sum.12
  398.9 0.2 broadcast_in_dim.9
  399.1 32.5 %all_to_all.17 = bf16[8,768,192]{1,2,0:T(8,128)(2,1)S(1)} all-to-all(bf16[8,768,192]{1,2,0:T(8,128)(2,1)S(1)} %broadcast_in_dim.9), channel_id=1, replica_groups=mesh['row'=8,'col'=32] {'row'}, dimensions={0} | all-to-all | bytes 4718592 | tf_op jit(solution)/shard_map/all_to_all | solution.py:15
  431.6 0.3 copy.16
  431.9 27.7 %all-gather.14.cloned.1.call-done = bf16[768,6144]{0,1:T(8,128)(2,1)} async-done(((bf16[768,192]{0,1:T(8,128)(2,1)}), bf16[768,6144]{0,1:T(8,128)(2,1)}) %all-gather.14.cloned.1.call-update) | async-done | bytes 9437200 | tf_op jit(solution)/shard_map/all_gather | solution.py:64
  459.6 6.4 %convolution_convert_fusion.2 = bf16[192,768]{1,0:T(8,128)(2,1)} fusion(bf16[6144,192]{0,1:T(8,128)(2,1)S(1)} %bitcast.20, bf16[768,6144]{0,1:T(8,128)(2,1)} %all-gather.14.cloned.1.call-done), kind=kOutput, calls=%fused_computation.3 | convolution fusion | flops 1812086784 | bytes 12091392 | tf_op jit(solution)/shard_map/dot_general | solution.py:63
  (10 shorter events, 0.1 us)
Async XLA Ops:
  6.5 109.5 %all-gather.6.cloned.1.call-start = ((), (), s32[]{:S(2)}) async-start(), calls=%async_computation.3 | async-start | bytes 9732096 | tf_op jit(solution)/shard_map/all_gather | solution.py:38
  7.3 137.1 %all-gather.10.cloned.1.call-start = ((), (), s32[]{:S(2)}) async-start(), calls=%async_computation.5 | async-start | bytes 2654208 | tf_op jit(solution)/shard_map/all_gather | solution.py:44
  8.0 241.5 %all-gather.8.cloned.1.call-start = ((), (), s32[]{:S(2)}) async-start(), calls=%async_computation.4 | async-start | bytes 9732096 | tf_op jit(solution)/shard_map/all_gather | solution.py:47
  116.1 133.4 %copy-start.1 = (f32[768]{0:T(1024)S(1)}, f32[768]{0:T(1024)}, u32[]{:S(2)}) copy-start(f32[768]{0:T(1024)} %param.8) | copy-start | bytes 9220
  116.1 133.4 %copy-start.2 = (f32[192]{0:T(256)S(1)}, f32[192]{0:T(256)}, u32[]{:S(2)}) copy-start(f32[192]{0:T(256)} %param.9) | copy-start | bytes 2308
  122.5 234.5 %copy-start = (bf16[192,768]{1,0:T(8,128)(2,1)S(1)}, bf16[192,768]{1,0:T(8,128)(2,1)}, u32[]{:S(2)}) copy-start(bf16[192,768]{1,0:T(8,128)(2,1)} %param.6) | copy-start | bytes 884740
  122.5 234.5 %all-gather.12.cloned.1.call-start = ((), (), s32[]{:S(2)}) async-start(), calls=%async_computation.6 | async-start | bytes 9732096 | tf_op jit(solution)/shard_map/all_gather | solution.py:52
  256.6 203.0 %all-gather.14.cloned.1.call-start = ((), (), s32[]{:S(2)}) async-start(), calls=%async_computation.7 | async-start | bytes 9732096 | tf_op jit(solution)/shard_map/all_gather | solution.py:64
Sparse Core Ops, SparseCore 0:
  9.9 106.1 all-gather.5
  117.9 26.3 all-gather.9
  146.9 102.5 all-gather.7
  256.7 100.1 all-gather.11
  359.4 100.1 all-gather.13
where the time goes:
time: 473 us
  waiting for transfers between devices  328 us (69%)
  blocking collectives  102 us (22%)
  matrix products  26.8 us (6%)
  between operations  13.2 us (3%)
    all_gather x1, waiting for transfers between devices, body(): lax.all_gather(projected, 'col', axis=1, tiled=True)  105 us
    all_gather x1, waiting for transfers between devices, body(): scaled_strip = lax.all_gather(scaled, 'col', axis=1, tiled=True)  99.8 us
    all_gather x1, waiting for transfers between devices, body(): lax.all_gather(basis_left, 'col', axis=0, tiled=True)  71.9 us
    all_to_all x2, blocking collectives, sent_to_all(): return lax.all_to_all(copies, axis, split_axis=0, concat_axis=0, tiled=True)  67.3 us
    all_to_all x1, blocking collectives, sent_and_summed(): parts = lax.all_to_all(in_blocks(shard, dim, peers), axis, 0, 0, tiled=True)  34.5 us
    all_gather x1, waiting for transfers between devices, body(): lax.all_gather(basis_right, 'col', axis=1, tiled=True)  27.7 us
    all_gather x1, waiting for transfers between devices, body(): right_strip = lax.all_gather(basis_right, 'row', axis=0, tiled=True)  21.8 us
  transfers between devices with their start and end apart: 5, of which 5 were waited for; matrix products, arithmetic and copies ran while one was open for 3% of the time, Pallas kernels for 0%

commit v1 on v0

--- a/solution.py
+++ b/solution.py
@@ -35,7 +35,9 @@
     c_strip = gathered_copies(rhs, "row", 0)
     chosen = c_strip
     first = lax.dot_general(
-        lax.all_gather(basis_left, "col", axis=0, tiled=True),
+        jnp.concatenate(
+            lax.all_to_all(jnp.stack([basis_left] * lax.axis_size("col")), "col", 0, 0), axis=0
+        ),
         chosen,
         (((0,), (0,)), ((), ())),
         preferred_element_type=jnp.float32,

time: 473 us -> 611 us (1.29)
  waiting for transfers between devices: 328 us -> 448 us
  starting transfers between devices: 0.16 us -> 11.3 us
  local copies, waits for them, and re-layouts: 1.97 us -> 8.14 us
    all_to_all x0 -> x1, waiting for transfers between devices: none -> 207 us  [body(): lax.all_to_all(jnp.stack([basis_left] * lax.axis_size('col')), 'col', 0, 0)]
    all_gather x1 -> x0, waiting for transfers between devices: 71.9 us -> none  [body(): lax.all_gather(basis_left, 'col', axis=0, tiled=True)]
    all_gather x1, waiting for transfers between devices: 21.8 us -> 0.02 us  [body(): right_strip = lax.all_gather(basis_right, 'row', axis=0, tiled=True)]
    all_to_all x0 -> x1, starting transfers between devices: none -> 11.1 us  [body(): lax.all_to_all(jnp.stack([basis_left] * lax.axis_size('col')), 'col', 0, 0)]
    all_gather x1, waiting for transfers between devices: 105 us -> 111 us  [body(): lax.all_gather(projected, 'col', axis=1, tiled=True)]
  transfers between devices with their start and end apart: 5 -> 5, of which waited for: 5 -> 4; matrix products, arithmetic and copies ran while one was open for 3% -> 3% of each run, Pallas kernels for 0% -> 0%
where the time goes in v1:
time: 611 us; the launch traced here: 610 us
  waiting for transfers between devices  448 us (73%)
  blocking collectives  102 us (17%)
  matrix products  27.5 us (5%)
  between operations  13.2 us (2%)
  starting transfers between devices  11.3 us (2%)
  local copies, waits for them, and re-layouts  8.14 us (1%)
    all_to_all x1, waiting for transfers between devices, body(): lax.all_to_all(jnp.stack([basis_left] * lax.axis_size('col')), 'col', 0, 0)  207 us
    all_gather x1, waiting for transfers between devices, body(): lax.all_gather(projected, 'col', axis=1, tiled=True)  111 us
    all_gather x1, waiting for transfers between devices, body(): scaled_strip = lax.all_gather(scaled, 'col', axis=1, tiled=True)  99.8 us
    all_to_all x2, blocking collectives, sent_to_all(): return lax.all_to_all(copies, axis, split_axis=0, concat_axis=0, tiled=True)  67.4 us
    all_to_all x1, blocking collectives, sent_and_summed(): parts = lax.all_to_all(in_blocks(shard, dim, peers), axis, 0, 0, tiled=True)  34.5 us
    all_gather x1, waiting for transfers between devices, body(): lax.all_gather(basis_right, 'col', axis=1, tiled=True)  27.7 us
  transfers between devices with their start and end apart: 5, of which 4 were waited for; matrix products, arithmetic and copies ran while one was open for 3% of the time, Pallas kernels for 0%

profile of v1, /device:TPU:1, one launch (start us, length us, event | category | flops | bytes accessed | tf_op | source)
XLA Modules:
  0.0 610.2 jit_solution(3107721417477762986)
XLA Ops:
  6.5 1.1 broadcast_in_dim.8
  7.7 34.9 %all_to_all.20 = bf16[8,768,192]{1,2,0:T(8,128)(2,1)S(1)} all-to-all(bf16[8,768,192]{1,2,0:T(8,128)(2,1)S(1)} %broadcast_in_dim.8), channel_id=1, replica_groups=mesh['row'=8,'col'=32] {'row'}, dimensions={0} | all-to-all | bytes 4718592 | tf_op jit(solution)/shard_map/all_to_all | solution.py:15
  42.5 4.7 stack.2
  47.2 11.1 %all-to-all-start = ((bf16[32,192,768]{2,1,0:T(8,128)(2,1)}), bf16[32,192,768]{2,1,0:T(8,128)(2,1)}, u32[]{:S(2)}, u32[]{:S(2)}) async-start(bf16[32,192,768]{2,1,0:T(8,128)(2,1)} %stack.2), calls=%async_computation | async-start | bytes 18874368 | tf_op jit(solution)/shard_map/all_to_all | solution.py:39
  58.4 0.0 all-gather.7.cloned.1.call-start
  58.5 0.7 all-gather.7.cloned.1.call-update
  59.2 1.7 copy.15
  60.9 207.5 %all-to-all-done = bf16[32,192,768]{2,1,0:T(8,128)(2,1)} async-done(((bf16[32,192,768]{2,1,0:T(8,128)(2,1)}), bf16[32,192,768]{2,1,0:T(8,128)(2,1)}, u32[]{:S(2)}, u32[]{:S(2)}) %all-to-all-start) | async-done | bytes 9437216 | tf_op jit(solution)/shard_map/all_to_all | solution.py:39
  268.4 7.1 %convolution_convert_fusion.1 = bf16[768,192]{0,1:T(8,128)(2,1)} fusion(bf16[6144,192]{0,1:T(8,128)(2,1)} %bitcast.20, bf16[6144,768]{1,0:T(8,128)(2,1)} %bitcast), kind=kOutput, calls=%fused_computation.2 | convolution fusion | flops 1812086784 | bytes 12091392 | tf_op jit(solution)/shard_map/dot_general | solution.py:37
  275.5 0.0 all-gather.9.cloned.1.call-start
  275.6 111.5 %all-gather.5.cloned.1.call-done = bf16[768,6144]{0,1:T(8,128)(2,1)} async-done(((bf16[768,192]{0,1:T(8,128)(2,1)}), bf16[768,6144]{0,1:T(8,128)(2,1)}) %all-gather.5.cloned.1.call-update) | async-done | bytes 9437200 | tf_op jit(solution)/shard_map/all_gather | solution.py:49
  387.1 7.1 %fusion = bf16[768,192]{0,1:T(8,128)(2,1)} fusion(bf16[6144,192]{0,1:T(8,128)(2,1)} %all-gather.7.cloned.1.call-done, bf16[768,6144]{0,1:T(8,128)(2,1)} %all-gather.5.cloned.1.call-done, f32[192]{0:T(256)S(1)} %copy-done.2, f32[768]{0:T(1024)S(1)} %copy-done.1), kind=kOutput, calls=%fused_computation.5 | convolution fusion | flops 1812381696 | bytes 12095232 | tf_op jit(solution)/shard_map/dot_general | solution.py:48
  394.3 0.0 all-gather.11.cloned.1.call-start
  394.3 0.5 all-gather.11.cloned.1.call-update
  394.8 99.8 %all-gather.9.cloned.1.call-done = bf16[768,6144]{0,1:T(8,128)(2,1)} async-done(((bf16[768,192]{0,1:T(8,128)(2,1)}), bf16[768,6144]{0,1:T(8,128)(2,1)}) %all-gather.9.cloned.1.call-update) | async-done | bytes 9437200 | tf_op jit(solution)/shard_map/all_gather | solution.py:54
  494.6 6.9 %convolution_convert_fusion = bf16[6144,192]{0,1:T(8,128)(2,1)S(1)} fusion(bf16[768,6144]{0,1:T(8,128)(2,1)} %all-gather.9.cloned.1.call-done, bf16[192,768]{1,0:T(8,128)(2,1)S(1)} %copy-done), kind=kOutput, calls=%fused_computation | convolution fusion | flops 1813118976 | bytes 12091392 | tf_op jit(solution)/shard_map/dot_general | solution.py:57
  501.5 0.2 copy.18
  501.7 34.5 %all_to_all.21 = bf16[8,768,192]{1,2,0:T(8,128)(2,1)S(1)} all-to-all(bf16[8,768,192]{1,2,0:T(8,128)(2,1)S(1)} %bitcast.18), channel_id=1, replica_groups=mesh['row'=8,'col'=32] {'row'}, dimensions={0} | all-to-all | bytes 4718592 | tf_op jit(solution)/shard_map/all_to_all | solution.py:30
  536.1 0.4 reduce_sum.12
  536.5 0.2 broadcast_in_dim.9
  536.7 32.5 %all_to_all.22 = bf16[8,768,192]{1,2,0:T(8,128)(2,1)S(1)} all-to-all(bf16[8,768,192]{1,2,0:T(8,128)(2,1)S(1)} %broadcast_in_dim.9), channel_id=1, replica_groups=mesh['row'=8,'col'=32] {'row'}, dimensions={0} | all-to-all | bytes 4718592 | tf_op jit(solution)/shard_map/all_to_all | solution.py:15
  569.2 0.3 copy.16
  569.5 27.7 %all-gather.11.cloned.1.call-done = bf16[768,6144]{0,1:T(8,128)(2,1)} async-done(((bf16[768,192]{0,1:T(8,128)(2,1)}), bf16[768,6144]{0,1:T(8,128)(2,1)}) %all-gather.11.cloned.1.call-update) | async-done | bytes 9437200 | tf_op jit(solution)/shard_map/all_gather | solution.py:66
  597.3 6.4 %convolution_convert_fusion.2 = bf16[192,768]{1,0:T(8,128)(2,1)} fusion(bf16[6144,192]{0,1:T(8,128)(2,1)S(1)} %bitcast.21, bf16[768,6144]{0,1:T(8,128)(2,1)} %all-gather.11.cloned.1.call-done), kind=kOutput, calls=%fused_computation.3 | convolution fusion | flops 1812086784 | bytes 12091392 | tf_op jit(solution)/shard_map/dot_general | solution.py:65
  (10 shorter events, 0.1 us)
Async XLA Ops:
  7.7 34.9 %copy-start = (bf16[192,768]{1,0:T(8,128)(2,1)S(1)}, bf16[192,768]{1,0:T(8,128)(2,1)}, u32[]{:S(2)}) copy-start(bf16[192,768]{1,0:T(8,128)(2,1)} %param.6) | copy-start | bytes 884740
  47.2 221.1 %all-to-all-start = ((bf16[32,192,768]{2,1,0:T(8,128)(2,1)}), bf16[32,192,768]{2,1,0:T(8,128)(2,1)}, u32[]{:S(2)}, u32[]{:S(2)}) async-start(bf16[32,192,768]{2,1,0:T(8,128)(2,1)} %stack.2), calls=%async_computation | async-start | bytes 18874368 | tf_op jit(solution)/shard_map/all_to_all | solution.py:39
  58.4 217.2 %all-gather.7.cloned.1.call-start = ((), (), s32[]{:S(2)}) async-start(), calls=%async_computation.5 | async-start | bytes 2654208 | tf_op jit(solution)/shard_map/all_gather | solution.py:46
  59.1 328.0 %all-gather.5.cloned.1.call-start = ((), (), s32[]{:S(2)}) async-start(), calls=%async_computation.4 | async-start | bytes 9732096 | tf_op jit(solution)/shard_map/all_gather | solution.py:49
  268.4 118.7 %copy-start.1 = (f32[768]{0:T(1024)S(1)}, f32[768]{0:T(1024)}, u32[]{:S(2)}) copy-start(f32[768]{0:T(1024)} %param.8) | copy-start | bytes 9220
  268.4 118.7 %copy-start.2 = (f32[192]{0:T(256)S(1)}, f32[192]{0:T(256)}, u32[]{:S(2)}) copy-start(f32[192]{0:T(256)} %param.9) | copy-start | bytes 2308
  275.5 219.1 %all-gather.9.cloned.1.call-start = ((), (), s32[]{:S(2)}) async-start(), calls=%async_computation.6 | async-start | bytes 9732096 | tf_op jit(solution)/shard_map/all_gather | solution.py:54
  394.3 203.0 %all-gather.11.cloned.1.call-start = ((), (), s32[]{:S(2)}) async-start(), calls=%async_computation.7 | async-start | bytes 9732096 | tf_op jit(solution)/shard_map/all_gather | solution.py:66
Sparse Core Ops, SparseCore 0:
  61.1 28.5 all-gather.6
  275.7 111.4 all-gather.4
  394.4 100.1 all-gather.8
  497.1 100.1 all-gather.10
